TPU v7x, 512 devices: a whole 4x8x8 slice. The times are simulated.
512 devices in a mesh: lon: 128 (over x_lo, z, y), lat: 4 (over x_hi, core).
Axes of the slice: x: 4 (x_hi: 2, x_lo: 2; x = x_hi * 2 + x_lo), y: 8, z: 8, core: 2. Of those that a mesh axis runs over, the one named last changes fastest.
Arguments:
- inverse: float32 [256, 8, 128, 128], P('lon', 'lat'), may hold values from -0.1 to 0.2
- vert_diag: float32 [256, 8, 128], P('lon', 'lat'), may hold values from 0.1 to 1
- vert_coup: float32 [256, 8, 128], P('lon', 'lat'), may hold values from 0.5 to 4
- face_east: float32 [256, 8, 128], P('lon', 'lat'), may hold values from 0.3 to 3
- face_north: float32 [256, 8, 128], P('lon', 'lat'), may hold values from 0.3 to 3
- land_mask: int32 [256, 8], P('lon', 'lat'), may hold values 0 or 1
- aggregate: int32 [256, 8], P('lon', 'lat'), may hold values from -1 to 511, as said below
Outputs:
- coarse: float32 [128, 4, 13, 128, 128], P('lon', 'lat')
Inputs may be any that keep to these rules, and one draw needn't show every extreme that they name: `aggregate`: each entry is -1 (the column belongs to no coarse column) or the index I * 4 + J of the coarse column (I, J) = (i // 2, j // 2) of its own 2 x 2 block; -1 may occur anywhere and is more frequent in the two fine latitudes nearest each end of the latitude range.
All inputs are finite; a program needn't handle non-finite values. No bound on the sum of `land_mask` on one device may be relied on, other than what follows from the above.
Results may differ from a plain program's by a relative error of at most 0.0002.
Values sent between devices are 32-bit elements; how exact they have to be, the bound alone decides.
A program may use at most 64 MiB of HBM per device.

v0:
```python
import jax
import jax.numpy as jnp
from jax import lax
from jax.experimental import pallas as pl
from jax.experimental.pallas import tpu as pltpu
from jax.sharding import PartitionSpec as P

MESH = pl.DeviceIdType.MESH
relax = 0.6
offsets = [
    (-2, 0),
    (-1, -1),
    (-1, 0),
    (-1, 1),
    (0, -2),
    (0, -1),
    (0, 0),
    (0, 1),
    (0, 2),
    (1, -1),
    (1, 0),
    (1, 1),
    (2, 0),
]
slot_of = {offset: place for place, offset in enumerate(offsets)}
near_blocks = [(0, 0), (1, 0), (-1, 0), (0, 1), (0, -1)]
second_blocks = [(2, 0), (-2, 0), (0, 2), (0, -2)]
corner_blocks = [(1, 1), (-1, 1), (1, -1), (-1, -1)]
sides = [(1, 0), (-1, 0), (0, 1), (0, -1)]


def corner_cell(block):
    return (0 if block[0] > 0 else 1, 0 if block[1] > 0 else 1)


def cells_of(block):
    return [(2 * block[0] + p, 2 * block[1] + r) for p in (0, 1) for r in (0, 1)]


def near_cells(side):
    a, b = side
    if b == 0:
        p = 0 if a > 0 else 1
        return [(2 * a + p, r) for r in (0, 1)]
    r = 0 if b > 0 else 1
    return [(p, 2 * b + r) for p in (0, 1)]


def far_cells(side):
    near = near_cells(side)
    return [cell for cell in cells_of(side) if cell not in near]


def neighbours(cell):
    x, y = cell
    return [(x + 1, y), (x - 1, y), (x, y + 1), (x, y - 1)]


own_cells = cells_of((0, 0))
support = own_cells + [cell for side in sides for cell in near_cells(side)]
outer = [cell for side in sides for cell in far_cells(side)] + [
    (2 * a + corner_cell((a, b))[0], 2 * b + corner_cell((a, b))[1]) for a, b in corner_blocks
]
all_cells = support + outer
cell_index = {cell: place for place, cell in enumerate(all_cells)}
COEFS = 9
edge_list = []
for cell in support:
    for other in neighbours(cell):
        key = tuple(sorted((cell, other)))
        if key not in edge_list:
            edge_list.append(key)
edge_index = {edge: COEFS * len(all_cells) + place for place, edge in enumerate(edge_list)}
coef_rows = COEFS * len(all_cells) + len(edge_list)
coef_rows = (coef_rows + 7) // 8 * 8

message = {}
for block in near_blocks[1:] + second_blocks + corner_blocks:
    message["packet", block] = len(message)
for side in sides:
    for cell in near_cells(side) + far_cells(side):
        message["block", cell] = len(message)
for block in corner_blocks:
    message["corner", block] = len(message)


def down(values):
    lane = lax.broadcasted_iota(jnp.int32, values.shape, 1)
    return jnp.where(lane > 0, pltpu.roll(values, 1, 1), 0.0)


def split(values):
    high = values.astype(jnp.bfloat16)
    low = (values - high.astype(jnp.float32)).astype(jnp.bfloat16)
    return high, low


def kernel(
    inv_h, vd_h, vc_h, fe_h, fn_h, land_h, agg_h,
    out,
    X, XC, PK, PC, PD, SD, SM, LA, PT, CF,
    local_sem, send_sem, recv_sem,
):
    me_lon = lax.axis_index("lon")
    me_lat = lax.axis_index("lat")
    count_lon = lax.axis_size("lon")
    count_lat = lax.axis_size("lat")
    own_of = {"vd": 0, "vc": 1, "fe": 2, "fn": 3}

    inverse_copy = pltpu.make_async_copy(inv_h, X.at[0], local_sem.at[0])
    small_copies = [
        pltpu.make_async_copy(source, SM.at[place], local_sem.at[1 + place])
        for place, source in enumerate((vd_h, vc_h, fe_h, fn_h))
    ] + [
        pltpu.make_async_copy(source, LA.at[place], local_sem.at[5 + place])
        for place, source in enumerate((land_h, agg_h))
    ]
    for copy in small_copies:
        copy.start()
    inverse_copy.start()

    def target(block):
        a, b = block
        return {"lon": lax.rem(me_lon + a + count_lon, count_lon), "lat": me_lat + b}

    def exists(block):
        b = block[1]
        if b == 0:
            return None
        return me_lat + b < count_lat if b > 0 else me_lat + b >= 0

    def only(condition, action):
        if condition is None:
            action()
        else:
            pl.when(condition)(action)

    partners = near_blocks[1:] + second_blocks + corner_blocks
    barrier = pltpu.get_barrier_semaphore()
    for block in partners:
        def signal(block=block):
            pl.semaphore_signal(barrier, inc=1, device_id=target(block), device_id_type=MESH)
        only(exists(block), signal)

    for block in partners:
        if block[1] == 0:
            continue
        def clear(block=block):
            if block in near_blocks:
                place = near_blocks.index(block)
                PK[place] = jnp.zeros((24, 128), jnp.float32)
                X[place] = jnp.zeros((2, 2, 128, 128), jnp.float32)
            elif block in second_blocks:
                PC[second_blocks.index(block)] = jnp.zeros((8, 128), jnp.float32)
            else:
                PD[corner_blocks.index(block)] = jnp.zeros((8, 128), jnp.float32)
                XC[corner_blocks.index(block)] = jnp.zeros((128, 128), jnp.float32)
        pl.when(jnp.logical_not(exists(block)))(clear)

    for copy in small_copies:
        copy.wait()
    live = (LA[1] >= 0).astype(jnp.float32)
    land = LA[0].astype(jnp.float32)

    def spread(values, p, r):
        return jnp.broadcast_to(values[p : p + 1, r : r + 1], (1, 128))

    lives = {(p, r): spread(live, p, r) for p in (0, 1) for r in (0, 1)}
    block_count = lives[0, 0] + lives[0, 1] + lives[1, 0] + lives[1, 1]
    norm = jnp.sqrt(jnp.maximum(block_count, 1.0))
    lane = lax.broadcasted_iota(jnp.int32, (1, 128), 1)
    scalars = jnp.zeros((1, 128), jnp.float32)
    for p in (0, 1):
        for r in (0, 1):
            scalars = jnp.where(lane == 2 * p + r, spread(land, p, r), scalars)
            scalars = jnp.where(lane == 4 + 2 * p + r, lives[p, r] / norm, scalars)

    def mine(field, p, r):
        return SM[own_of[field], p, pl.ds(r, 1), :]

    blank = jnp.zeros((1, 128), jnp.float32)
    head = [scalars, mine("fe", 1, 0), mine("fe", 1, 1), mine("fn", 0, 1), mine("fn", 1, 1)]
    for row, values in enumerate(head + [blank] * 3):
        PK[0, pl.ds(row, 1), :] = values
    for first, field in ((8, "fe"), (12, "fn"), (16, "vd"), (20, "vc")):
        for p in (0, 1):
            for r in (0, 1):
                PK[0, pl.ds(first + 2 * p + r, 1), :] = mine(field, p, r)
    lands = {(p, r): spread(land, p, r) for p in (0, 1) for r in (0, 1)}
    for place, block in enumerate(corner_blocks):
        p, r = corner_cell(block)
        east = mine("fe", 0, r) * (lands[0, r] * lands[1, r])
        north = mine("fn", p, 0) * (lands[p, 0] * lands[p, 1])
        vc = mine("vc", p, r)
        inner = lives[p, r] / norm * (mine("vd", p, r) + vc + down(vc) + east + north)
        inner = inner - (east * (lives[1 - p, r] / norm) + north * (lives[p, 1 - r] / norm))
        for row, values in enumerate(head + [inner, vc, blank]):
            SD[place, pl.ds(row, 1), :] = values

    lat_near = jnp.where(me_lat + 1 < count_lat, 3, 0) + jnp.where(me_lat >= 1, 3, 0)
    lat_second = jnp.where(me_lat + 2 < count_lat, 1, 0) + jnp.where(me_lat >= 2, 1, 0)
    pl.semaphore_wait(barrier, 4 + lat_near + lat_second)

    def move(key, source, landing, block):
        place = message[key]
        return pltpu.make_async_remote_copy(
            src_ref=source,
            dst_ref=landing,
            send_sem=send_sem.at[place],
            recv_sem=recv_sem.at[place],
            device_id=target(block),
            device_id_type=MESH,
        )

    def opposite(block):
        return (-block[0], -block[1])

    sends = []

    def send(key, source, landing, block, condition):
        copy = move(key, source, landing, block)
        only(condition, copy.start)
        sends.append((copy, condition))

    def packet_landing(block):
        if block in near_blocks:
            return PK.at[near_blocks.index(block)]
        if block in second_blocks:
            return PC.at[second_blocks.index(block)]
        return PD.at[corner_blocks.index(block)]

    def packet_source(block):
        if block in near_blocks:
            return PK.at[0]
        if block in second_blocks:
            return PK.at[0, pl.ds(0, 8)]
        return SD.at[corner_blocks.index(block)]

    for block in partners:
        goal = opposite(block)
        send(("packet", block), packet_source(block), packet_landing(block), goal, exists(goal))

    def block_ref(cell):
        x, y = cell
        block = (x // 2, y // 2)
        if block in near_blocks:
            return X.at[near_blocks.index(block), x % 2, y % 2]
        return XC.at[corner_blocks.index(block)]

    def block_value(cell):
        x, y = cell
        block = (x // 2, y // 2)
        if block in near_blocks:
            return X[near_blocks.index(block), x % 2, y % 2]
        return XC[corner_blocks.index(block)]

    inverse_copy.wait()
    for cells in (near_cells, far_cells):
        for step in (0, 1):
            for side in sides:
                cell = cells(side)[step]
                goal = opposite(side)
                source = X.at[0, cell[0] % 2, cell[1] % 2]
                send(("block", cell), source, block_ref(cell), goal, exists(goal))

    def wait_packet(block):
        copy = move(("packet", block), packet_source(block), packet_landing(block), block)
        only(exists(block), copy.wait_recv)

    def wait_block(cell):
        block = (cell[0] // 2, cell[1] // 2)
        copy = move(("block", cell), X.at[0, 0, 0], block_ref(cell), block)
        only(exists(block), copy.wait_recv)

    cache = {}

    def field(name, cell):
        if (name, cell) in cache:
            return cache[name, cell]
        x, y = cell
        block = (x // 2, y // 2)
        p, r = x % 2, y % 2
        place = 2 * p + r
        if block in near_blocks:
            ref, at = PK, near_blocks.index(block)
            row = {"fe": 8, "fn": 12, "vd": 16, "vc": 20}.get(name, 0) + place
        else:
            if block in second_blocks:
                ref, at = PC, second_blocks.index(block)
            else:
                ref, at = PD, corner_blocks.index(block)
            if name == "fe":
                assert p == 1
                row = 1 + r
            elif name == "fn":
                assert r == 1
                row = 3 + p
            elif name in ("inner", "vc"):
                assert (p, r) == corner_cell(block)
                row = 5 if name == "inner" else 6
        if name in ("land", "w"):
            lane_at = place + (4 if name == "w" else 0)
            row_values = ref[at, pl.ds(0, 1), :]
            value = jnp.broadcast_to(row_values[:, lane_at : lane_at + 1], (1, 128))
        else:
            value = ref[at, pl.ds(row, 1), :]
        cache[name, cell] = value
        return value

    def face(low, high):
        if ("face", low, high) not in cache:
            name = "fe" if low[1] == high[1] else "fn"
            cache["face", low, high] = field(name, low) * (field("land", low) * field("land", high))
        return cache["face", low, high]

    def between(cell, other):
        return face(*sorted((cell, other)))

    def coef(cell, row):
        return CF[pl.ds(COEFS * cell_index[cell] + row, 1), :]

    def edge(cell, other):
        return CF[pl.ds(edge_index[tuple(sorted((cell, other)))], 1), :]

    top = lax.broadcasted_iota(jnp.int32, (1, 128), 1) < 127

    def make_coefs(cell):
        x, y = cell
        p, r = x % 2, y % 2
        lon_cross, lon_same = ((x - 1, y), (x + 1, y)) if p == 0 else ((x + 1, y), (x - 1, y))
        lat_cross, lat_same = ((x, y - 1), (x, y + 1)) if r == 0 else ((x, y + 1), (x, y - 1))
        w = field("w", cell)
        vc = field("vc", cell)
        if abs(x // 2) + abs(y // 2) == 2 and x // 2 and y // 2:
            crossing = between(cell, lon_cross) + between(cell, lat_cross)
            weighted = field("inner", cell) + w * crossing
        else:
            main = field("vd", cell) + vc + down(vc)
            for other in neighbours(cell):
                main = main + between(cell, other)
            same = between(cell, lon_same) * field("w", lon_same)
            same = same + between(cell, lat_same) * field("w", lat_same)
            weighted = w * main - same
        up = jnp.where(top, vc, 0.0)
        below = down(up)
        rows = [
            w,
            -relax * weighted,
            relax * w * below,
            relax * w * up,
            relax * between(cell, lon_cross) * field("w", lon_cross),
            relax * between(cell, lat_cross) * field("w", lat_cross),
        ]
        if cell in support:
            rows += [main, -below, -up]
        for row, values in enumerate(rows):
            CF[pl.ds(COEFS * cell_index[cell] + row, 1), :] = values

    for block in near_blocks[1:]:
        wait_packet(block)
    for cell in own_cells:
        make_coefs(cell)

    def roll_down(values):
        return pltpu.roll(values, 1, 1)

    def roll_up(values):
        return pltpu.roll(values, 127, 1)

    diagonal = lax.broadcasted_iota(jnp.int32, (128, 128), 0) == lax.broadcasted_iota(
        jnp.int32, (128, 128), 1
    )
    for cell in own_cells:
        inverse = block_value(cell)
        values = jnp.where(diagonal, coef(cell, 0), 0.0) + inverse * coef(cell, 1)
        values = values + roll_down(inverse) * coef(cell, 2) + roll_up(inverse) * coef(cell, 3)
        PT[cell_index[cell]] = values.T

    for block in second_blocks + corner_blocks:
        wait_packet(block)
    for cell in all_cells:
        if cell not in own_cells:
            make_coefs(cell)
    for low, high in edge_list:
        CF[pl.ds(edge_index[low, high], 1), :] = face(low, high)

    def relay(condition, source_cell, corner, goal):
        def start():
            move(("corner", corner), block_ref(source_cell), XC.at[corner_blocks.index(corner)], goal).start()
        pl.when(condition)(start)
        sends.append((move(("corner", corner), block_ref(source_cell), XC.at[0], goal), condition))

    even = lax.rem(me_lat, 2) == 0
    odd = lax.rem(me_lat, 2) == 1
    lat_up = jnp.logical_and(odd, me_lat + 1 < count_lat)
    lat_down = jnp.logical_and(even, me_lat >= 1)

    def near_columns(side):
        for cell in near_cells(side):
            wait_block(cell)
        a, b = side
        if b == 0:
            x = 2 if a > 0 else -1
            relay(even, (x, 1), (a, -1), (0, 1))
            relay(odd, (x, 0), (a, 1), (0, -1))
        elif b == 1:
            relay(lat_up, (1, 2), (-1, 1), (1, 0))
            relay(lat_up, (0, 2), (1, 1), (-1, 0))
        else:
            relay(lat_down, (1, -1), (-1, -1), (1, 0))
            relay(lat_down, (0, -1), (1, -1), (-1, 0))
        for cell in near_cells(side):
            row = 4 if b == 0 else 5
            PT[cell_index[cell]] = (block_value(cell) * coef(cell, row)).T

    filled = set()

    def add(block, values):
        place = slot_of[block]
        if place in filled:
            out[place] = out[place] + values
        else:
            out[place] = values
            filled.add(place)

    def galerkin(cell):
        x, y = cell
        a, b = x // 2, y // 2
        applied = None
        if cell in support:
            own = PT[cell_index[cell]]
            applied = own * coef(cell, 6) + roll_down(own) * coef(cell, 7) + roll_up(own) * coef(cell, 8)
        for other in neighbours(cell):
            if other in support:
                term = PT[cell_index[other]] * edge(cell, other)
                applied = -term if applied is None else applied - term
        high, low = split(applied)
        left = jnp.concatenate([high, low], axis=1)
        high, low = split(block_value(cell))
        right = jnp.concatenate([high, low], axis=1)
        right = jnp.concatenate([right, right], axis=0)
        product = jnp.dot(left, right, preferred_element_type=jnp.float32)
        product = product[:, :128] + product[:, 128:]
        own = applied * coef(cell, 0) + product * coef(cell, 1)
        own = own + roll_down(product) * coef(cell, 2) + roll_up(product) * coef(cell, 3)
        add((a, b), own)
        add((a + (1 if x % 2 else -1), b), product * coef(cell, 4))
        add((a, b + (1 if y % 2 else -1)), product * coef(cell, 5))

    for side in sides:
        near_columns(side)
    for cell in support:
        galerkin(cell)
    for step in (0, 1):
        for side in sides:
            cell = far_cells(side)[step]
            wait_block(cell)
            galerkin(cell)
    for block in corner_blocks:
        p, r = corner_cell(block)
        cell = (2 * block[0] + p, 2 * block[1] + r)
        landing = XC.at[corner_blocks.index(block)]
        copy = move(("corner", block), X.at[0, 0, 0], landing, (block[0], 0))
        pl.when(exists(block))(copy.wait_recv)
        galerkin(cell)
    assert len(filled) == len(offsets)
    for copy, condition in sends:
        only(condition, copy.wait_send)


def local(inverse, vert_diag, vert_coup, face_east, face_north, land_mask, aggregate):
    blocks = len(offsets)
    messages = len(message)
    coarse = pl.pallas_call(
        kernel,
        out_shape=jax.ShapeDtypeStruct((blocks, 128, 128), jnp.float32),
        in_specs=[pl.BlockSpec(memory_space=pl.ANY)] * 7,
        out_specs=pl.BlockSpec(memory_space=pltpu.VMEM),
        scratch_shapes=[
            pltpu.VMEM((5, 2, 2, 128, 128), jnp.float32),
            pltpu.VMEM((4, 128, 128), jnp.float32),
            pltpu.VMEM((5, 24, 128), jnp.float32),
            pltpu.VMEM((4, 8, 128), jnp.float32),
            pltpu.VMEM((4, 8, 128), jnp.float32),
            pltpu.VMEM((4, 8, 128), jnp.float32),
            pltpu.VMEM((4, 2, 2, 128), jnp.float32),
            pltpu.VMEM((2, 2, 2), jnp.int32),
            pltpu.VMEM((len(support), 128, 128), jnp.float32),
            pltpu.VMEM((coef_rows, 128), jnp.float32),
            pltpu.SemaphoreType.DMA((7,)),
            pltpu.SemaphoreType.DMA((messages,)),
            pltpu.SemaphoreType.DMA((messages,)),
        ],
        compiler_params=pltpu.CompilerParams(collective_id=0, has_side_effects=True),
    )(inverse, vert_diag, vert_coup, face_east, face_north, land_mask, aggregate)
    return coarse[None, None]


def solution(mesh):
    return jax.shard_map(
        local,
        mesh=mesh,
        in_specs=(
            P("lon", "lat", None, None),
            P("lon", "lat", None),
            P("lon", "lat", None),
            P("lon", "lat", None),
            P("lon", "lat", None),
            P("lon", "lat"),
            P("lon", "lat"),
        ),
        out_specs=P("lon", "lat", None, None, None),
        check_vma=False,
    )
```

profile of v0, /device:TPU:1, one launch (start us, length us, event | category | flops | bytes accessed | tf_op | source)
XLA Modules:
  0.0 35.3 jit_solution(12652047813541992865)
XLA Ops:
  0.0 33.2 %shard_map.73 = f32[13,128,128]{2,1,0:T(8,128)} custom-call(f32[2,2,128,128]{3,2,1,0:T(8,128)} %inv_h.1, f32[2,2,128]{2,1,0:T(2,128)} %vd_h.1, f32[2,2,128]{2,1,0:T(2,128)} %vc_h.1, f32[2,2,128]{2,1,0:T(2,128)} %fe_h.1, f32[2,2,128]{2,1,0:T(2,128)} %fn_h.1, s32[2,2]{1,0:T(2,128)} %land_h.1, s32[2,2]{1,0:T(2,128)} %agg_h.1), custom_call_target="tpu_custom_call" | custom-call | tf_op jit(solution)/shard_map/pallas_call | solution.py:474
  33.2 2.1 %copy.9 = f32[1,1,13,128,128]{4,3,2,1,0:T(8,128)} copy(f32[1,1,13,128,128]{4,3,2,1,0:T(8,128)} %bitcast.1) | data formatting | bytes 1703936
where the time goes:
time: 35.5 us; the launch traced here: 35.3 us
  Pallas kernels  33.2 us (94%)
  local copies, waits for them, and re-layouts  2.12 us (6%)
    pallas_call x1, Pallas kernels, local(): pl.pallas_call(kernel, out_shape=jax.ShapeDtypeStruct((blocks, 128, 128),...  33.2 us
    unnamed x1, local copies, waits for them, and re-layouts  2.12 us

commit v1 on v0

--- a/solution.py
+++ b/solution.py
@@ -26,6 +26,7 @@
 near_blocks = [(0, 0), (1, 0), (-1, 0), (0, 1), (0, -1)]
 second_blocks = [(2, 0), (-2, 0), (0, 2), (0, -2)]
 corner_blocks = [(1, 1), (-1, 1), (1, -1), (-1, -1)]
+packet_blocks = near_blocks + corner_blocks
 sides = [(1, 0), (-1, 0), (0, 1), (0, -1)]
 
 
@@ -98,7 +99,7 @@
 def kernel(
     inv_h, vd_h, vc_h, fe_h, fn_h, land_h, agg_h,
     out,
-    X, XC, PK, PC, PD, SD, SM, LA, PT, CF,
+    X, XC, PK, PC, SM, LA, PT, CF,
     local_sem, send_sem, recv_sem,
 ):
     me_lon = lax.axis_index("lon")
@@ -106,8 +107,8 @@
     count_lon = lax.axis_size("lon")
     count_lat = lax.axis_size("lat")
     own_of = {"vd": 0, "vc": 1, "fe": 2, "fn": 3}
-
-    inverse_copy = pltpu.make_async_copy(inv_h, X.at[0], local_sem.at[0])
+    east, west, north, south = sides
+
     small_copies = [
         pltpu.make_async_copy(source, SM.at[place], local_sem.at[1 + place])
         for place, source in enumerate((vd_h, vc_h, fe_h, fn_h))
@@ -115,6 +116,7 @@
         pltpu.make_async_copy(source, LA.at[place], local_sem.at[5 + place])
         for place, source in enumerate((land_h, agg_h))
     ]
+    inverse_copy = pltpu.make_async_copy(inv_h, X.at[0], local_sem.at[0])
     for copy in small_copies:
         copy.start()
     inverse_copy.start()
@@ -129,31 +131,35 @@
             return None
         return me_lat + b < count_lat if b > 0 else me_lat + b >= 0
 
+    def both(first, second):
+        if first is None:
+            return second
+        return first if second is None else jnp.logical_and(first, second)
+
     def only(condition, action):
         if condition is None:
             action()
         else:
             pl.when(condition)(action)
 
-    partners = near_blocks[1:] + second_blocks + corner_blocks
     barrier = pltpu.get_barrier_semaphore()
-    for block in partners:
+    for block in (west, north, south):
         def signal(block=block):
             pl.semaphore_signal(barrier, inc=1, device_id=target(block), device_id_type=MESH)
         only(exists(block), signal)
 
+    partners = near_blocks[1:] + second_blocks + corner_blocks
     for block in partners:
         if block[1] == 0:
             continue
         def clear(block=block):
+            if block in second_blocks:
+                PC[second_blocks.index(block)] = jnp.zeros((8, 128), jnp.float32)
+                return
+            PK[packet_blocks.index(block)] = jnp.zeros((24, 128), jnp.float32)
             if block in near_blocks:
-                place = near_blocks.index(block)
-                PK[place] = jnp.zeros((24, 128), jnp.float32)
-                X[place] = jnp.zeros((2, 2, 128, 128), jnp.float32)
-            elif block in second_blocks:
-                PC[second_blocks.index(block)] = jnp.zeros((8, 128), jnp.float32)
+                X[near_blocks.index(block)] = jnp.zeros((2, 2, 128, 128), jnp.float32)
             else:
-                PD[corner_blocks.index(block)] = jnp.zeros((8, 128), jnp.float32)
                 XC[corner_blocks.index(block)] = jnp.zeros((128, 128), jnp.float32)
         pl.when(jnp.logical_not(exists(block)))(clear)
 
@@ -186,20 +192,11 @@
         for p in (0, 1):
             for r in (0, 1):
                 PK[0, pl.ds(first + 2 * p + r, 1), :] = mine(field, p, r)
-    lands = {(p, r): spread(land, p, r) for p in (0, 1) for r in (0, 1)}
-    for place, block in enumerate(corner_blocks):
-        p, r = corner_cell(block)
-        east = mine("fe", 0, r) * (lands[0, r] * lands[1, r])
-        north = mine("fn", p, 0) * (lands[p, 0] * lands[p, 1])
-        vc = mine("vc", p, r)
-        inner = lives[p, r] / norm * (mine("vd", p, r) + vc + down(vc) + east + north)
-        inner = inner - (east * (lives[1 - p, r] / norm) + north * (lives[p, 1 - r] / norm))
-        for row, values in enumerate(head + [inner, vc, blank]):
-            SD[place, pl.ds(row, 1), :] = values
-
-    lat_near = jnp.where(me_lat + 1 < count_lat, 3, 0) + jnp.where(me_lat >= 1, 3, 0)
-    lat_second = jnp.where(me_lat + 2 < count_lat, 1, 0) + jnp.where(me_lat >= 2, 1, 0)
-    pl.semaphore_wait(barrier, 4 + lat_near + lat_second)
+
+    lat_count = jnp.where(me_lat + 1 < count_lat, 1, 0) + jnp.where(me_lat >= 1, 1, 0)
+    pl.semaphore_wait(barrier, 1 + lat_count)
+
+    sends = []
 
     def move(key, source, landing, block):
         place = message[key]
@@ -215,30 +212,10 @@
     def opposite(block):
         return (-block[0], -block[1])
 
-    sends = []
-
-    def send(key, source, landing, block, condition):
-        copy = move(key, source, landing, block)
-        only(condition, copy.start)
-        sends.append((copy, condition))
-
-    def packet_landing(block):
-        if block in near_blocks:
-            return PK.at[near_blocks.index(block)]
+    def packet_ref(block):
         if block in second_blocks:
             return PC.at[second_blocks.index(block)]
-        return PD.at[corner_blocks.index(block)]
-
-    def packet_source(block):
-        if block in near_blocks:
-            return PK.at[0]
-        if block in second_blocks:
-            return PK.at[0, pl.ds(0, 8)]
-        return SD.at[corner_blocks.index(block)]
-
-    for block in partners:
-        goal = opposite(block)
-        send(("packet", block), packet_source(block), packet_landing(block), goal, exists(goal))
+        return PK.at[packet_blocks.index(block)]
 
     def block_ref(cell):
         x, y = cell
@@ -254,23 +231,72 @@
             return X[near_blocks.index(block), x % 2, y % 2]
         return XC[corner_blocks.index(block)]
 
+    def corner_of(block):
+        p, r = corner_cell(block)
+        return (2 * block[0] + p, 2 * block[1] + r)
+
+    def send(key, source, landing, goal, condition):
+        copy = move(key, source, landing, goal)
+        only(condition, copy.start)
+        sends.append((copy, condition))
+        return copy
+
+    def send_packet(goal):
+        seen = opposite(goal)
+        send(("packet", seen), PK.at[0], packet_ref(seen), goal, exists(goal))
+
+    def send_blocks(goal, cells):
+        seen = opposite(goal)
+        for cell in cells(seen):
+            source = X.at[0, cell[0] % 2, cell[1] % 2]
+            send(("block", cell), source, block_ref(cell), goal, exists(goal))
+
+    def relay_packet(block):
+        for goal in sides:
+            if goal == block or (block[0] == 0 and goal[1] == 0):
+                continue
+            seen = (block[0] - goal[0], block[1] - goal[1])
+            condition = both(exists(block), exists(goal))
+            source = packet_ref(block)
+            if seen in second_blocks:
+                source = PK.at[packet_blocks.index(block), pl.ds(0, 8)]
+            send(("packet", seen), source, packet_ref(seen), goal, condition)
+
+    def relay_corners(block):
+        for goal in (north, south):
+            seen = (block[0], -goal[1])
+            cell = corner_of(seen)
+            source = block_ref((cell[0], cell[1] + 2 * goal[1]))
+            send(("corner", seen), source, block_ref(cell), goal, exists(goal))
+
+    def wait(key, source, landing, origin, condition):
+        only(condition, move(key, source, landing, origin).wait_recv)
+
+    def wait_packet(block, origin=None):
+        landing = packet_ref(block)
+        source = PK.at[0, pl.ds(0, 8)] if block in second_blocks else PK.at[0]
+        wait(("packet", block), source, landing, origin or block, exists(block))
+
+    def wait_block(cell):
+        block = (cell[0] // 2, cell[1] // 2)
+        wait(("block", cell), X.at[0, 0, 0], block_ref(cell), block, exists(block))
+
+    for goal in (east, north, south):
+        send_packet(goal)
     inverse_copy.wait()
     for cells in (near_cells, far_cells):
-        for step in (0, 1):
-            for side in sides:
-                cell = cells(side)[step]
-                goal = opposite(side)
-                source = X.at[0, cell[0] % 2, cell[1] % 2]
-                send(("block", cell), source, block_ref(cell), goal, exists(goal))
-
-    def wait_packet(block):
-        copy = move(("packet", block), packet_source(block), packet_landing(block), block)
-        only(exists(block), copy.wait_recv)
-
-    def wait_block(cell):
-        block = (cell[0] // 2, cell[1] // 2)
-        copy = move(("block", cell), X.at[0, 0, 0], block_ref(cell), block)
-        only(exists(block), copy.wait_recv)
+        send_blocks(east, cells)
+    for cells in (near_cells, far_cells):
+        for goal in (north, south):
+            send_blocks(goal, cells)
+    wait_packet(west)
+    send_packet(west)
+    for cells in (near_cells, far_cells):
+        send_blocks(west, cells)
+    for block in (west, east, north, south):
+        if block != west:
+            wait_packet(block)
+        relay_packet(block)
 
     cache = {}
 
@@ -281,23 +307,13 @@
         block = (x // 2, y // 2)
         p, r = x % 2, y % 2
         place = 2 * p + r
-        if block in near_blocks:
-            ref, at = PK, near_blocks.index(block)
+        if block in second_blocks:
+            ref, at = PC, second_blocks.index(block)
+            row = {"fe": 1 + r, "fn": 3 + p}.get(name, 0)
+            assert (name != "fe" or p == 1) and (name != "fn" or r == 1)
+        else:
+            ref, at = PK, packet_blocks.index(block)
             row = {"fe": 8, "fn": 12, "vd": 16, "vc": 20}.get(name, 0) + place
-        else:
-            if block in second_blocks:
-                ref, at = PC, second_blocks.index(block)
-            else:
-                ref, at = PD, corner_blocks.index(block)
-            if name == "fe":
-                assert p == 1
-                row = 1 + r
-            elif name == "fn":
-                assert r == 1
-                row = 3 + p
-            elif name in ("inner", "vc"):
-                assert (p, r) == corner_cell(block)
-                row = 5 if name == "inner" else 6
         if name in ("land", "w"):
             lane_at = place + (4 if name == "w" else 0)
             row_values = ref[at, pl.ds(0, 1), :]
@@ -331,16 +347,12 @@
         lat_cross, lat_same = ((x, y - 1), (x, y + 1)) if r == 0 else ((x, y + 1), (x, y - 1))
         w = field("w", cell)
         vc = field("vc", cell)
-        if abs(x // 2) + abs(y // 2) == 2 and x // 2 and y // 2:
-            crossing = between(cell, lon_cross) + between(cell, lat_cross)
-            weighted = field("inner", cell) + w * crossing
-        else:
-            main = field("vd", cell) + vc + down(vc)
-            for other in neighbours(cell):
-                main = main + between(cell, other)
-            same = between(cell, lon_same) * field("w", lon_same)
-            same = same + between(cell, lat_same) * field("w", lat_same)
-            weighted = w * main - same
+        main = field("vd", cell) + vc + down(vc)
+        for other in neighbours(cell):
+            main = main + between(cell, other)
+        same = between(cell, lon_same) * field("w", lon_same)
+        same = same + between(cell, lat_same) * field("w", lat_same)
+        weighted = w * main - same
         up = jnp.where(top, vc, 0.0)
         below = down(up)
         rows = [
@@ -356,8 +368,6 @@
         for row, values in enumerate(rows):
             CF[pl.ds(COEFS * cell_index[cell] + row, 1), :] = values
 
-    for block in near_blocks[1:]:
-        wait_packet(block)
     for cell in own_cells:
         make_coefs(cell)
 
@@ -376,41 +386,24 @@
         values = values + roll_down(inverse) * coef(cell, 2) + roll_up(inverse) * coef(cell, 3)
         PT[cell_index[cell]] = values.T
 
-    for block in second_blocks + corner_blocks:
-        wait_packet(block)
+    for block in second_blocks[:1] + second_blocks[2:]:
+        wait_packet(block, (block[0] // 2, block[1] // 2))
+    for block in corner_blocks:
+        wait_packet(block, (0, block[1]))
+    late_cells = far_cells(west)
     for cell in all_cells:
-        if cell not in own_cells:
+        if cell not in own_cells and cell not in late_cells:
             make_coefs(cell)
     for low, high in edge_list:
         CF[pl.ds(edge_index[low, high], 1), :] = face(low, high)
 
-    def relay(condition, source_cell, corner, goal):
-        def start():
-            move(("corner", corner), block_ref(source_cell), XC.at[corner_blocks.index(corner)], goal).start()
-        pl.when(condition)(start)
-        sends.append((move(("corner", corner), block_ref(source_cell), XC.at[0], goal), condition))
-
-    even = lax.rem(me_lat, 2) == 0
-    odd = lax.rem(me_lat, 2) == 1
-    lat_up = jnp.logical_and(odd, me_lat + 1 < count_lat)
-    lat_down = jnp.logical_and(even, me_lat >= 1)
-
     def near_columns(side):
         for cell in near_cells(side):
             wait_block(cell)
-        a, b = side
-        if b == 0:
-            x = 2 if a > 0 else -1
-            relay(even, (x, 1), (a, -1), (0, 1))
-            relay(odd, (x, 0), (a, 1), (0, -1))
-        elif b == 1:
-            relay(lat_up, (1, 2), (-1, 1), (1, 0))
-            relay(lat_up, (0, 2), (1, 1), (-1, 0))
-        else:
-            relay(lat_down, (1, -1), (-1, -1), (1, 0))
-            relay(lat_down, (0, -1), (1, -1), (-1, 0))
+        if side in (east, west):
+            relay_corners(side)
         for cell in near_cells(side):
-            row = 4 if b == 0 else 5
+            row = 4 if side in (east, west) else 5
             PT[cell_index[cell]] = (block_value(cell) * coef(cell, row)).T
 
     filled = set()
@@ -447,41 +440,66 @@
         add((a + (1 if x % 2 else -1), b), product * coef(cell, 4))
         add((a, b + (1 if y % 2 else -1)), product * coef(cell, 5))
 
-    for side in sides:
+    def corner(block):
+        landing = XC.at[corner_blocks.index(block)]
+        wait(("corner", block), X.at[0, 0, 0], landing, (0, block[1]), exists(block))
+        galerkin(corner_of(block))
+
+    for side in (east, north, south):
         near_columns(side)
-    for cell in support:
+    for side in (east, north, south):
+        for cell in near_cells(side):
+            galerkin(cell)
+    for cell in own_cells[2:]:
         galerkin(cell)
-    for step in (0, 1):
-        for side in sides:
-            cell = far_cells(side)[step]
+    for side in (east, north, south):
+        for cell in far_cells(side):
             wait_block(cell)
             galerkin(cell)
     for block in corner_blocks:
-        p, r = corner_cell(block)
-        cell = (2 * block[0] + p, 2 * block[1] + r)
-        landing = XC.at[corner_blocks.index(block)]
-        copy = move(("corner", block), X.at[0, 0, 0], landing, (block[0], 0))
-        pl.when(exists(block))(copy.wait_recv)
+        if block[0] > 0:
+            corner(block)
+    near_columns(west)
+    for cell in own_cells[:2] + near_cells(west):
         galerkin(cell)
+    wait_packet((-2, 0), west)
+    for cell in late_cells:
+        make_coefs(cell)
+    for cell in late_cells:
+        wait_block(cell)
+        galerkin(cell)
+    for block in corner_blocks:
+        if block[0] < 0:
+            corner(block)
     assert len(filled) == len(offsets)
     for copy, condition in sends:
         only(condition, copy.wait_send)
 
 
+def publish(held, out, sem):
+    copies = [
+        pltpu.make_async_copy(held.at[place], out.at[place], sem.at[place])
+        for place in range(len(offsets))
+    ]
+    for copy in copies:
+        copy.start()
+    for copy in copies:
+        copy.wait()
+
+
 def local(inverse, vert_diag, vert_coup, face_east, face_north, land_mask, aggregate):
     blocks = len(offsets)
     messages = len(message)
-    coarse = pl.pallas_call(
+    anywhere = pl.BlockSpec(memory_space=pltpu.HBM)
+    held = pl.pallas_call(
         kernel,
-        out_shape=jax.ShapeDtypeStruct((blocks, 128, 128), jnp.float32),
-        in_specs=[pl.BlockSpec(memory_space=pl.ANY)] * 7,
+        out_shape=pltpu.VMEM((blocks, 128, 128), jnp.float32),
+        in_specs=[anywhere] * 7,
         out_specs=pl.BlockSpec(memory_space=pltpu.VMEM),
         scratch_shapes=[
             pltpu.VMEM((5, 2, 2, 128, 128), jnp.float32),
             pltpu.VMEM((4, 128, 128), jnp.float32),
-            pltpu.VMEM((5, 24, 128), jnp.float32),
-            pltpu.VMEM((4, 8, 128), jnp.float32),
-            pltpu.VMEM((4, 8, 128), jnp.float32),
+            pltpu.VMEM((9, 24, 128), jnp.float32),
             pltpu.VMEM((4, 8, 128), jnp.float32),
             pltpu.VMEM((4, 2, 2, 128), jnp.float32),
             pltpu.VMEM((2, 2, 2), jnp.int32),
@@ -493,6 +511,14 @@
         ],
         compiler_params=pltpu.CompilerParams(collective_id=0, has_side_effects=True),
     )(inverse, vert_diag, vert_coup, face_east, face_north, land_mask, aggregate)
+    coarse = pl.pallas_call(
+        publish,
+        out_shape=jax.ShapeDtypeStruct((blocks, 128, 128), jnp.float32),
+        in_specs=[pl.BlockSpec(memory_space=pltpu.VMEM)],
+        out_specs=anywhere,
+        scratch_shapes=[pltpu.SemaphoreType.DMA((blocks,))],
+        compiler_params=pltpu.CompilerParams(vmem_limit_bytes=2**20),
+    )(held)
     return coarse[None, None]
 
 

time: 35.5 us -> 33.7 us (0.949)
  local copies, waits for them, and re-layouts: 2.12 us -> 0 us
  Pallas kernels: 33.2 us -> 33.6 us
    unnamed x1 -> x0, local copies, waits for them, and re-layouts: 2.12 us -> none
    pallas_call x1 -> x2, Pallas kernels: 33.2 us -> 33.6 us  [the longest x1 32.6 us: local(): pl.pallas_call(kernel, out_shape=pltpu.VMEM((blocks, 128, 128), jnp.float...]
where the time goes in v1:
time: 33.7 us; the launch traced here: 33.6 us
  Pallas kernels  33.6 us (100%)
    pallas_call x1, Pallas kernels, local(): pl.pallas_call(kernel, out_shape=pltpu.VMEM((blocks, 128, 128), jnp.float...  32.6 us
    pallas_call x1, Pallas kernels, local(): pl.pallas_call(publish, out_shape=jax.ShapeDtypeStruct((blocks, 128, 128)...  1 us

profile of v1, /device:TPU:1, one launch (start us, length us, event | category | flops | bytes accessed | tf_op | source)
XLA Modules:
  0.0 33.6 jit_solution(17214288601025266232)
XLA Ops:
  0.0 32.6 %shard_map.73.held = f32[13,128,128]{2,1,0:T(8,128)S(1)} custom-call(f32[2,2,128,128]{3,2,1,0:T(8,128)} %inv_h.1, f32[2,2,128]{2,1,0:T(2,128)} %vd_h.1, f32[2,2,128]{2,1,0:T(2,128)} %vc_h.1, f32[2,2,128]{2,1,0:T(2,128)} %fe_h.1, f32[2,2,128]{2,1,0:T(2,128)} %fn_h.1, s32[2,2]{1,0:T(2,128)} %land_h.1, s32[2,2]{1,0:T(2,128)} %agg_h.1), custom_call_target="tpu_custom_call" | custom-call | tf_op jit(solution)/shard_map/pallas_call | solution.py:494
  32.6 1.0 %shard_map.74 = f32[13,128,128]{2,1,0:T(8,128)} custom-call(f32[13,128,128]{2,1,0:T(8,128)S(1)} %shard_map.73.held), custom_call_target="tpu_custom_call" | custom-call | tf_op jit(solution)/shard_map/pallas_call | solution.py:514

commit v2 on v1

--- a/solution.py
+++ b/solution.py
@@ -125,11 +125,10 @@
         a, b = block
         return {"lon": lax.rem(me_lon + a + count_lon, count_lon), "lat": me_lat + b}
 
+    inside = {b: me_lat + b < count_lat if b > 0 else me_lat + b >= 0 for b in (-2, -1, 1, 2)}
+
     def exists(block):
-        b = block[1]
-        if b == 0:
-            return None
-        return me_lat + b < count_lat if b > 0 else me_lat + b >= 0
+        return inside.get(block[1])
 
     def both(first, second):
         if first is None:
@@ -142,11 +141,21 @@
         else:
             pl.when(condition)(action)
 
+    phase = lax.rem(me_lon, 64)
+    late = phase == 0
+    early = jnp.logical_not(late)
+    even = lax.rem(me_lat, 2) == 0
+    odd = lax.rem(me_lat, 2) == 1
+    across_up = jnp.logical_and(odd, me_lat + 1 < count_lat)
+    across_down = jnp.logical_and(even, me_lat >= 1)
     barrier = pltpu.get_barrier_semaphore()
-    for block in (west, north, south):
+    for block in near_blocks[1:] + second_blocks + corner_blocks:
+        reach = None
+        if block[0] > 0:
+            reach = phase < 64 - block[0]
         def signal(block=block):
             pl.semaphore_signal(barrier, inc=1, device_id=target(block), device_id_type=MESH)
-        only(exists(block), signal)
+        only(both(exists(block), reach), signal)
 
     partners = near_blocks[1:] + second_blocks + corner_blocks
     for block in partners:
@@ -193,8 +202,10 @@
             for r in (0, 1):
                 PK[0, pl.ds(first + 2 * p + r, 1), :] = mine(field, p, r)
 
-    lat_count = jnp.where(me_lat + 1 < count_lat, 1, 0) + jnp.where(me_lat >= 1, 1, 0)
-    pl.semaphore_wait(barrier, 1 + lat_count)
+    lat_near = jnp.where(inside[1], 1, 0) + jnp.where(inside[-1], 1, 0)
+    lat_second = jnp.where(inside[2], 1, 0) + jnp.where(inside[-2], 1, 0)
+    awaited = 2 + 2 * lat_near + lat_second + jnp.where(early, 1 + lat_near, 0)
+    pl.semaphore_wait(barrier, awaited + jnp.where(phase > 1, 1, 0))
 
     sends = []
 
@@ -235,68 +246,73 @@
         p, r = corner_cell(block)
         return (2 * block[0] + p, 2 * block[1] + r)
 
+    listed = set()
+
     def send(key, source, landing, goal, condition):
         copy = move(key, source, landing, goal)
         only(condition, copy.start)
-        sends.append((copy, condition))
-        return copy
-
-    def send_packet(goal):
+        if (key, goal) not in listed:
+            sends.append((key, goal, exists(goal) if key[0] != "corner" else condition))
+            listed.add((key, goal))
+
+    def send_packet(goal, condition=None):
         seen = opposite(goal)
-        send(("packet", seen), PK.at[0], packet_ref(seen), goal, exists(goal))
-
-    def send_blocks(goal, cells):
+        source = PK.at[0, pl.ds(0, 8)] if seen in second_blocks else PK.at[0]
+        send(("packet", seen), source, packet_ref(seen), goal, both(exists(goal), condition))
+
+    def send_blocks(goal, cells, condition=None):
         seen = opposite(goal)
         for cell in cells(seen):
             source = X.at[0, cell[0] % 2, cell[1] % 2]
-            send(("block", cell), source, block_ref(cell), goal, exists(goal))
-
-    def relay_packet(block):
-        for goal in sides:
-            if goal == block or (block[0] == 0 and goal[1] == 0):
-                continue
-            seen = (block[0] - goal[0], block[1] - goal[1])
-            condition = both(exists(block), exists(goal))
-            source = packet_ref(block)
-            if seen in second_blocks:
-                source = PK.at[packet_blocks.index(block), pl.ds(0, 8)]
-            send(("packet", seen), source, packet_ref(seen), goal, condition)
+            send(("block", cell), source, block_ref(cell), goal, both(exists(goal), condition))
+
+    def mate(goal):
+        return even if goal == north else odd
 
     def relay_corners(block):
         for goal in (north, south):
             seen = (block[0], -goal[1])
             cell = corner_of(seen)
             source = block_ref((cell[0], cell[1] + 2 * goal[1]))
-            send(("corner", seen), source, block_ref(cell), goal, exists(goal))
+            condition = mate(goal) if block == west else exists(goal)
+            send(("corner", seen), source, block_ref(cell), goal, condition)
+
+    def send_across(goal, condition):
+        seen = opposite(goal)
+        cell = corner_of(seen)
+        source = X.at[0, cell[0] % 2, cell[1] % 2]
+        send(("corner", seen), source, block_ref(cell), goal, condition)
 
     def wait(key, source, landing, origin, condition):
         only(condition, move(key, source, landing, origin).wait_recv)
 
-    def wait_packet(block, origin=None):
+    def wait_packet(block):
         landing = packet_ref(block)
         source = PK.at[0, pl.ds(0, 8)] if block in second_blocks else PK.at[0]
-        wait(("packet", block), source, landing, origin or block, exists(block))
+        wait(("packet", block), source, landing, block, exists(block))
 
     def wait_block(cell):
         block = (cell[0] // 2, cell[1] // 2)
         wait(("block", cell), X.at[0, 0, 0], block_ref(cell), block, exists(block))
 
-    for goal in (east, north, south):
+    def serve(goal, condition=None):
+        for cells in (near_cells, far_cells):
+            send_blocks(goal, cells, condition)
+
+    west_side = [west, (-1, 1), (-1, -1)]
+    for goal in (east, (2, 0), (1, 1), (1, -1), north, south, (0, 2), (0, -2)):
         send_packet(goal)
+    for goal in west_side:
+        send_packet(goal, early)
+    send_packet((-2, 0), phase > 1)
     inverse_copy.wait()
+    send_across((1, 1), across_up)
+    send_across((1, -1), across_down)
+    serve(east)
     for cells in (near_cells, far_cells):
-        send_blocks(east, cells)
-    for cells in (near_cells, far_cells):
-        for goal in (north, south):
-            send_blocks(goal, cells)
-    wait_packet(west)
-    send_packet(west)
-    for cells in (near_cells, far_cells):
-        send_blocks(west, cells)
-    for block in (west, east, north, south):
-        if block != west:
-            wait_packet(block)
-        relay_packet(block)
+        send_blocks(west, cells, early)
+        send_blocks(north, cells)
+        send_blocks(south, cells)
 
     cache = {}
 
@@ -368,9 +384,6 @@
         for row, values in enumerate(rows):
             CF[pl.ds(COEFS * cell_index[cell] + row, 1), :] = values
 
-    for cell in own_cells:
-        make_coefs(cell)
-
     def roll_down(values):
         return pltpu.roll(values, 1, 1)
 
@@ -380,31 +393,24 @@
     diagonal = lax.broadcasted_iota(jnp.int32, (128, 128), 0) == lax.broadcasted_iota(
         jnp.int32, (128, 128), 1
     )
-    for cell in own_cells:
-        inverse = block_value(cell)
-        values = jnp.where(diagonal, coef(cell, 0), 0.0) + inverse * coef(cell, 1)
-        values = values + roll_down(inverse) * coef(cell, 2) + roll_up(inverse) * coef(cell, 3)
-        PT[cell_index[cell]] = values.T
-
-    for block in second_blocks[:1] + second_blocks[2:]:
-        wait_packet(block, (block[0] // 2, block[1] // 2))
-    for block in corner_blocks:
-        wait_packet(block, (0, block[1]))
-    late_cells = far_cells(west)
-    for cell in all_cells:
-        if cell not in own_cells and cell not in late_cells:
-            make_coefs(cell)
-    for low, high in edge_list:
-        CF[pl.ds(edge_index[low, high], 1), :] = face(low, high)
+
+    def own_columns(cells):
+        for cell in cells:
+            inverse = block_value(cell)
+            values = jnp.where(diagonal, coef(cell, 0), 0.0) + inverse * coef(cell, 1)
+            values = values + roll_down(inverse) * coef(cell, 2) + roll_up(inverse) * coef(cell, 3)
+            PT[cell_index[cell]] = values.T
 
     def near_columns(side):
         for cell in near_cells(side):
-            wait_block(cell)
-        if side in (east, west):
-            relay_corners(side)
-        for cell in near_cells(side):
-            row = 4 if side in (east, west) else 5
-            PT[cell_index[cell]] = (block_value(cell) * coef(cell, row)).T
+            inner = (cell[0] - side[0], cell[1] - side[1])
+            scale = relax * between(cell, inner) * field("w", inner)
+            PT[cell_index[cell]] = (block_value(cell) * scale).T
+
+    def edges(early):
+        for low, high in edge_list:
+            if (high[0] >= 0 and low[0] >= 0) == early:
+                CF[pl.ds(edge_index[low, high], 1), :] = face(low, high)
 
     filled = set()
 
@@ -445,35 +451,67 @@
         wait(("corner", block), X.at[0, 0, 0], landing, (0, block[1]), exists(block))
         galerkin(corner_of(block))
 
-    for side in (east, north, south):
+    for block in (east, (2, 0), (1, 1), (1, -1), north, south, (0, 2), (0, -2)):
+        wait_packet(block)
+    for cell in all_cells:
+        if cell[0] > 0:
+            make_coefs(cell)
+    edges(True)
+    own_columns(own_cells[2:])
+    for side in (north, south, east):
+        for cell in near_cells(side):
+            wait_block(cell)
+        if side == east:
+            relay_corners(side)
         near_columns(side)
-    for side in (east, north, south):
-        for cell in near_cells(side):
-            galerkin(cell)
-    for cell in own_cells[2:]:
+    for cell in near_cells(east):
         galerkin(cell)
-    for side in (east, north, south):
+    for side in (north, south):
+        galerkin(near_cells(side)[1])
         for cell in far_cells(side):
             wait_block(cell)
-            galerkin(cell)
+        galerkin(far_cells(side)[1])
+    for cell in far_cells(east):
+        wait_block(cell)
+        galerkin(cell)
     for block in corner_blocks:
         if block[0] > 0:
             corner(block)
+
+    for block in west_side + [(-2, 0)]:
+        wait_packet(block)
+        send_packet(block, phase <= 1 if block == (-2, 0) else late)
+    for cell in all_cells:
+        if cell[0] <= 0:
+            make_coefs(cell)
+    edges(False)
+    own_columns(own_cells[:2])
+    for cell in own_cells[2:]:
+        galerkin(cell)
+    for side in (north, south):
+        for cell in (near_cells(side)[0], far_cells(side)[0]):
+            galerkin(cell)
+    for cell in near_cells(west):
+        wait_block(cell)
+    relay_corners(west)
+    serve(west, late)
     near_columns(west)
     for cell in own_cells[:2] + near_cells(west):
         galerkin(cell)
-    wait_packet((-2, 0), west)
-    for cell in late_cells:
-        make_coefs(cell)
-    for cell in late_cells:
+    for cell in far_cells(west):
         wait_block(cell)
         galerkin(cell)
     for block in corner_blocks:
         if block[0] < 0:
             corner(block)
     assert len(filled) == len(offsets)
-    for copy, condition in sends:
-        only(condition, copy.wait_send)
+    for key, goal, condition in sends:
+        def drain(key=key, goal=goal):
+            source = X.at[0, 0, 0]
+            if key[0] == "packet":
+                source = PK.at[0, pl.ds(0, 8)] if key[1] in second_blocks else PK.at[0]
+            move(key, source, source, goal).wait_send()
+        only(condition, drain)
 
 
 def publish(held, out, sem):

time: 33.7 us -> 30.2 us (0.90)
  Pallas kernels: 33.6 us -> 30 us
    pallas_call x1, Pallas kernels: 32.6 us -> 29 us  [local(): pl.pallas_call(kernel, out_shape=pltpu.VMEM((blocks, 128, 128), jnp.float...]
where the time goes in v2:
time: 30.2 us; the launch traced here: 30 us
  Pallas kernels  30 us (99%)
    pallas_call x1, Pallas kernels, local(): pl.pallas_call(kernel, out_shape=pltpu.VMEM((blocks, 128, 128), jnp.float...  29 us
    pallas_call x1, Pallas kernels, local(): pl.pallas_call(publish, out_shape=jax.ShapeDtypeStruct((blocks, 128, 128)...  1 us

profile of v2, /device:TPU:1, one launch (start us, length us, event | category | flops | bytes accessed | tf_op | source)
XLA Modules:
  0.0 30.0 jit_solution(7310816929600223192)
XLA Ops:
  0.0 29.0 %shard_map.73.held = f32[13,128,128]{2,1,0:T(8,128)S(1)} custom-call(f32[2,2,128,128]{3,2,1,0:T(8,128)} %inv_h.1, f32[2,2,128]{2,1,0:T(2,128)} %vd_h.1, f32[2,2,128]{2,1,0:T(2,128)} %vc_h.1, f32[2,2,128]{2,1,0:T(2,128)} %fe_h.1, f32[2,2,128]{2,1,0:T(2,128)} %fn_h.1, s32[2,2]{1,0:T(2,128)} %land_h.1, s32[2,2]{1,0:T(2,128)} %agg_h.1), custom_call_target="tpu_custom_call" | custom-call | tf_op jit(solution)/shard_map/pallas_call | solution.py:532
  29.0 1.0 %shard_map.74 = f32[13,128,128]{2,1,0:T(8,128)} custom-call(f32[13,128,128]{2,1,0:T(8,128)S(1)} %shard_map.73.held), custom_call_target="tpu_custom_call" | custom-call | tf_op jit(solution)/shard_map/pallas_call | solution.py:552

commit v3 on v2

--- a/solution.py
+++ b/solution.py
@@ -143,7 +143,8 @@
 
     phase = lax.rem(me_lon, 64)
     late = phase == 0
-    early = jnp.logical_not(late)
+    rim = phase == 63
+    inner = phase < 63
     even = lax.rem(me_lat, 2) == 0
     odd = lax.rem(me_lat, 2) == 1
     across_up = jnp.logical_and(odd, me_lat + 1 < count_lat)
@@ -152,7 +153,13 @@
     for block in near_blocks[1:] + second_blocks + corner_blocks:
         reach = None
         if block[0] > 0:
-            reach = phase < 64 - block[0]
+            reach = phase < 63 - block[0]
+        elif block == (0, 1):
+            reach = jnp.logical_or(inner, odd)
+        elif block == (0, -1):
+            reach = jnp.logical_or(inner, odd)
+        elif block == (0, -2):
+            reach = inner
         def signal(block=block):
             pl.semaphore_signal(barrier, inc=1, device_id=target(block), device_id_type=MESH)
         only(both(exists(block), reach), signal)
@@ -204,8 +211,10 @@
 
     lat_near = jnp.where(inside[1], 1, 0) + jnp.where(inside[-1], 1, 0)
     lat_second = jnp.where(inside[2], 1, 0) + jnp.where(inside[-2], 1, 0)
-    awaited = 2 + 2 * lat_near + lat_second + jnp.where(early, 1 + lat_near, 0)
-    pl.semaphore_wait(barrier, awaited + jnp.where(phase > 1, 1, 0))
+    from_west = jnp.where(late, 0, 1 + lat_near) + jnp.where(phase > 1, 1, 0)
+    awaited_inner = lat_near + lat_second + from_west
+    awaited_rim = jnp.where(even, lat_near, 0) + jnp.where(inside[-2], 1, 0)
+    pl.semaphore_wait(barrier, 2 + lat_near + jnp.where(rim, awaited_rim, awaited_inner))
 
     sends = []
 
@@ -286,10 +295,10 @@
     def wait(key, source, landing, origin, condition):
         only(condition, move(key, source, landing, origin).wait_recv)
 
-    def wait_packet(block):
+    def wait_packet(block, condition=None):
         landing = packet_ref(block)
         source = PK.at[0, pl.ds(0, 8)] if block in second_blocks else PK.at[0]
-        wait(("packet", block), source, landing, block, exists(block))
+        wait(("packet", block), source, landing, block, both(exists(block), condition))
 
     def wait_block(cell):
         block = (cell[0] // 2, cell[1] // 2)
@@ -300,19 +309,37 @@
             send_blocks(goal, cells, condition)
 
     west_side = [west, (-1, 1), (-1, -1)]
-    for goal in (east, (2, 0), (1, 1), (1, -1), north, south, (0, 2), (0, -2)):
+    free_west = jnp.logical_and(phase > 0, inner)
+    free_second = jnp.logical_and(phase > 1, inner)
+    held_lat = jnp.logical_and(rim, odd)
+    free_lat = jnp.logical_not(held_lat)
+    for goal in (east, (2, 0), (1, 1), (1, -1)):
         send_packet(goal)
-    for goal in west_side:
-        send_packet(goal, early)
-    send_packet((-2, 0), phase > 1)
     inverse_copy.wait()
     send_across((1, 1), across_up)
     send_across((1, -1), across_down)
+    for goal in west_side:
+        send_packet(goal, free_west)
+    send_packet((-2, 0), free_second)
+    send_packet(north, free_lat)
+    send_packet(south, free_lat)
+    send_packet((0, 2), inner)
+    send_packet((0, -2))
     serve(east)
     for cells in (near_cells, far_cells):
-        send_blocks(west, cells, early)
-        send_blocks(north, cells)
-        send_blocks(south, cells)
+        send_blocks(west, cells, free_west)
+        send_blocks(north, cells, free_lat)
+        send_blocks(south, cells, free_lat)
+    for block in (north, south):
+        wait_packet(block, held_lat)
+        send_packet(block, held_lat)
+        serve(block, held_lat)
+    for block in [(0, 2)] + west_side:
+        wait_packet(block, rim)
+        send_packet(block, rim)
+    serve(west, rim)
+    wait_packet((-2, 0), rim)
+    send_packet((-2, 0), rim)
 
     cache = {}
 
@@ -451,8 +478,11 @@
         wait(("corner", block), X.at[0, 0, 0], landing, (0, block[1]), exists(block))
         galerkin(corner_of(block))
 
-    for block in (east, (2, 0), (1, 1), (1, -1), north, south, (0, 2), (0, -2)):
+    for block in (east, (2, 0), (1, 1), (1, -1), (0, -2)):
         wait_packet(block)
+    wait_packet(north, free_lat)
+    wait_packet(south, free_lat)
+    wait_packet((0, 2), inner)
     for cell in all_cells:
         if cell[0] > 0:
             make_coefs(cell)
@@ -479,7 +509,7 @@
             corner(block)
 
     for block in west_side + [(-2, 0)]:
-        wait_packet(block)
+        wait_packet(block, inner)
         send_packet(block, phase <= 1 if block == (-2, 0) else late)
     for cell in all_cells:
         if cell[0] <= 0:

time: 30.2 us -> 27.8 us (0.921)
  Pallas kernels: 30 us -> 27.7 us
    pallas_call x1, Pallas kernels: 29 us -> 26.7 us  [local(): pl.pallas_call(kernel, out_shape=pltpu.VMEM((blocks, 128, 128), jnp.float...]
where the time goes in v3:
time: 27.8 us; the launch traced here: 27.7 us
  Pallas kernels  27.7 us (100%)
    pallas_call x1, Pallas kernels, local(): pl.pallas_call(kernel, out_shape=pltpu.VMEM((blocks, 128, 128), jnp.float...  26.7 us
    pallas_call x1, Pallas kernels, local(): pl.pallas_call(publish, out_shape=jax.ShapeDtypeStruct((blocks, 128, 128)...  1 us

profile of v3, /device:TPU:1, one launch (start us, length us, event | category | flops | bytes accessed | tf_op | source)
XLA Modules:
  0.0 27.7 jit_solution(3597983023404669628)
XLA Ops:
  0.0 26.7 %shard_map.73.held = f32[13,128,128]{2,1,0:T(8,128)S(1)} custom-call(f32[2,2,128,128]{3,2,1,0:T(8,128)} %inv_h.1, f32[2,2,128]{2,1,0:T(2,128)} %vd_h.1, f32[2,2,128]{2,1,0:T(2,128)} %vc_h.1, f32[2,2,128]{2,1,0:T(2,128)} %fe_h.1, f32[2,2,128]{2,1,0:T(2,128)} %fn_h.1, s32[2,2]{1,0:T(2,128)} %land_h.1, s32[2,2]{1,0:T(2,128)} %agg_h.1), custom_call_target="tpu_custom_call" | custom-call | tf_op jit(solution)/shard_map/pallas_call | solution.py:562
  26.7 1.0 %shard_map.74 = f32[13,128,128]{2,1,0:T(8,128)} custom-call(f32[13,128,128]{2,1,0:T(8,128)S(1)} %shard_map.73.held), custom_call_target="tpu_custom_call" | custom-call | tf_op jit(solution)/shard_map/pallas_call | solution.py:582

commit v4 on v3

--- a/solution.py
+++ b/solution.py
@@ -256,12 +256,13 @@
         return (2 * block[0] + p, 2 * block[1] + r)
 
     listed = set()
+    drains = {}
 
     def send(key, source, landing, goal, condition):
         copy = move(key, source, landing, goal)
         only(condition, copy.start)
         if (key, goal) not in listed:
-            sends.append((key, goal, exists(goal) if key[0] != "corner" else condition))
+            sends.append((key, goal))
             listed.add((key, goal))
 
     def send_packet(goal, condition=None):
@@ -275,22 +276,25 @@
             source = X.at[0, cell[0] % 2, cell[1] % 2]
             send(("block", cell), source, block_ref(cell), goal, both(exists(goal), condition))
 
-    def mate(goal):
-        return even if goal == north else odd
-
-    def relay_corners(block):
-        for goal in (north, south):
-            seen = (block[0], -goal[1])
-            cell = corner_of(seen)
-            source = block_ref((cell[0], cell[1] + 2 * goal[1]))
-            condition = mate(goal) if block == west else exists(goal)
-            send(("corner", seen), source, block_ref(cell), goal, condition)
+    def pass_near(side, condition=None):
+        for cell in near_cells(side):
+            wait_block(cell, condition)
+            if side in (east, west):
+                goal = north if cell[1] else south
+                seen = (side[0], -goal[1])
+                landing = block_ref(corner_of(seen))
+                facing = exists(goal)
+                if side == west:
+                    facing = even if goal == north else odd
+                send(("corner", seen), block_ref(cell), landing, goal, both(facing, condition))
+                drains["corner", seen, goal] = facing
 
     def send_across(goal, condition):
         seen = opposite(goal)
         cell = corner_of(seen)
         source = X.at[0, cell[0] % 2, cell[1] % 2]
         send(("corner", seen), source, block_ref(cell), goal, condition)
+        drains["corner", seen, goal] = condition
 
     def wait(key, source, landing, origin, condition):
         only(condition, move(key, source, landing, origin).wait_recv)
@@ -300,9 +304,10 @@
         source = PK.at[0, pl.ds(0, 8)] if block in second_blocks else PK.at[0]
         wait(("packet", block), source, landing, block, both(exists(block), condition))
 
-    def wait_block(cell):
+    def wait_block(cell, condition=None):
         block = (cell[0] // 2, cell[1] // 2)
-        wait(("block", cell), X.at[0, 0, 0], block_ref(cell), block, exists(block))
+        arrived = both(exists(block), condition)
+        wait(("block", cell), X.at[0, 0, 0], block_ref(cell), block, arrived)
 
     def serve(goal, condition=None):
         for cells in (near_cells, far_cells):
@@ -488,11 +493,9 @@
             make_coefs(cell)
     edges(True)
     own_columns(own_cells[2:])
-    for side in (north, south, east):
-        for cell in near_cells(side):
-            wait_block(cell)
-        if side == east:
-            relay_corners(side)
+    pass_near(west, jnp.logical_not(late))
+    for side in (east, north, south):
+        pass_near(side)
         near_columns(side)
     for cell in near_cells(east):
         galerkin(cell)
@@ -511,6 +514,8 @@
     for block in west_side + [(-2, 0)]:
         wait_packet(block, inner)
         send_packet(block, phase <= 1 if block == (-2, 0) else late)
+        if block == west:
+            send_blocks(west, near_cells, late)
     for cell in all_cells:
         if cell[0] <= 0:
             make_coefs(cell)
@@ -521,10 +526,8 @@
     for side in (north, south):
         for cell in (near_cells(side)[0], far_cells(side)[0]):
             galerkin(cell)
-    for cell in near_cells(west):
-        wait_block(cell)
-    relay_corners(west)
-    serve(west, late)
+    pass_near(west, late)
+    send_blocks(west, far_cells, late)
     near_columns(west)
     for cell in own_cells[:2] + near_cells(west):
         galerkin(cell)
@@ -535,13 +538,13 @@
         if block[0] < 0:
             corner(block)
     assert len(filled) == len(offsets)
-    for key, goal, condition in sends:
+    for key, goal in sends:
         def drain(key=key, goal=goal):
             source = X.at[0, 0, 0]
             if key[0] == "packet":
                 source = PK.at[0, pl.ds(0, 8)] if key[1] in second_blocks else PK.at[0]
             move(key, source, source, goal).wait_send()
-        only(condition, drain)
+        only(drains.get(key + (goal,), exists(goal)), drain)
 
 
 def publish(held, out, sem):

time: 27.8 us -> 25.9 us (0.932)
  Pallas kernels: 27.7 us -> 25.8 us
    pallas_call x1, Pallas kernels: 26.7 us -> 24.8 us  [local(): pl.pallas_call(kernel, out_shape=pltpu.VMEM((blocks, 128, 128), jnp.float...]
where the time goes in v4:
time: 25.9 us; the launch traced here: 25.8 us
  Pallas kernels  25.8 us (100%)
    pallas_call x1, Pallas kernels, local(): pl.pallas_call(kernel, out_shape=pltpu.VMEM((blocks, 128, 128), jnp.float...  24.8 us
    pallas_call x1, Pallas kernels, local(): pl.pallas_call(publish, out_shape=jax.ShapeDtypeStruct((blocks, 128, 128)...  1 us

profile of v4, /device:TPU:1, one launch (start us, length us, event | category | flops | bytes accessed | tf_op | source)
XLA Modules:
  0.0 25.8 jit_solution(7183870565233493270)
XLA Ops:
  0.0 24.8 %shard_map.73.held = f32[13,128,128]{2,1,0:T(8,128)S(1)} custom-call(f32[2,2,128,128]{3,2,1,0:T(8,128)} %inv_h.1, f32[2,2,128]{2,1,0:T(2,128)} %vd_h.1, f32[2,2,128]{2,1,0:T(2,128)} %vc_h.1, f32[2,2,128]{2,1,0:T(2,128)} %fe_h.1, f32[2,2,128]{2,1,0:T(2,128)} %fn_h.1, s32[2,2]{1,0:T(2,128)} %land_h.1, s32[2,2]{1,0:T(2,128)} %agg_h.1), custom_call_target="tpu_custom_call" | custom-call | tf_op jit(solution)/shard_map/pallas_call | solution.py:565
  24.8 1.0 %shard_map.74 = f32[13,128,128]{2,1,0:T(8,128)} custom-call(f32[13,128,128]{2,1,0:T(8,128)S(1)} %shard_map.73.held), custom_call_target="tpu_custom_call" | custom-call | tf_op jit(solution)/shard_map/pallas_call | solution.py:585

commit v5 on v4

--- a/solution.py
+++ b/solution.py
@@ -276,18 +276,28 @@
             source = X.at[0, cell[0] % 2, cell[1] % 2]
             send(("block", cell), source, block_ref(cell), goal, both(exists(goal), condition))
 
+    def pass_block(side, cell, condition):
+        wait_block(cell, condition)
+        if side not in (east, west):
+            return
+        goal = north if cell[1] else south
+        seen = (side[0], -goal[1])
+        landing = block_ref(corner_of(seen))
+        facing = exists(goal)
+        if side == west:
+            facing = even if goal == north else odd
+        send(("corner", seen), block_ref(cell), landing, goal, both(facing, condition))
+        drains["corner", seen, goal] = facing
+
     def pass_near(side, condition=None):
-        for cell in near_cells(side):
-            wait_block(cell, condition)
-            if side in (east, west):
-                goal = north if cell[1] else south
-                seen = (side[0], -goal[1])
-                landing = block_ref(corner_of(seen))
-                facing = exists(goal)
-                if side == west:
-                    facing = even if goal == north else odd
-                send(("corner", seen), block_ref(cell), landing, goal, both(facing, condition))
-                drains["corner", seen, goal] = facing
+        first, second = near_cells(side)
+        if side == west:
+            pass_block(side, second, both(condition, even))
+            pass_block(side, first, condition)
+            pass_block(side, second, both(condition, odd))
+        else:
+            pass_block(side, first, condition)
+            pass_block(side, second, condition)
 
     def send_across(goal, condition):
         seen = opposite(goal)
@@ -330,19 +340,25 @@
     send_packet(south, free_lat)
     send_packet((0, 2), inner)
     send_packet((0, -2))
-    serve(east)
+    send_blocks(east, lambda seen: near_cells(seen)[1:], even)
+    send_blocks(east, lambda seen: near_cells(seen)[:1])
+    send_blocks(east, lambda seen: near_cells(seen)[1:], odd)
+    send_blocks(east, far_cells)
     for cells in (near_cells, far_cells):
         send_blocks(west, cells, free_west)
         send_blocks(north, cells, free_lat)
         send_blocks(south, cells, free_lat)
+    wait_packet(west, rim)
+    send_packet(west, rim)
+    send_blocks(west, near_cells, rim)
     for block in (north, south):
         wait_packet(block, held_lat)
         send_packet(block, held_lat)
         serve(block, held_lat)
-    for block in [(0, 2)] + west_side:
+    for block in [(0, 2)] + west_side[1:]:
         wait_packet(block, rim)
         send_packet(block, rim)
-    serve(west, rim)
+    send_blocks(west, far_cells, rim)
     wait_packet((-2, 0), rim)
     send_packet((-2, 0), rim)
 
@@ -531,12 +547,12 @@
     near_columns(west)
     for cell in own_cells[:2] + near_cells(west):
         galerkin(cell)
+    for block in corner_blocks:
+        if block[0] < 0:
+            corner(block)
     for cell in far_cells(west):
         wait_block(cell)
         galerkin(cell)
-    for block in corner_blocks:
-        if block[0] < 0:
-            corner(block)
     assert len(filled) == len(offsets)
     for key, goal in sends:
         def drain(key=key, goal=goal):

time: 25.9 us -> 25.4 us (0.981)
  Pallas kernels: 25.8 us -> 25.3 us
    pallas_call x1, Pallas kernels: 24.8 us -> 24.3 us  [local(): pl.pallas_call(kernel, out_shape=pltpu.VMEM((blocks, 128, 128), jnp.float...]
where the time goes in v5:
time: 25.4 us; the launch traced here: 25.3 us
  Pallas kernels  25.3 us (100%)
    pallas_call x1, Pallas kernels, local(): pl.pallas_call(kernel, out_shape=pltpu.VMEM((blocks, 128, 128), jnp.float...  24.3 us
    pallas_call x1, Pallas kernels, local(): pl.pallas_call(publish, out_shape=jax.ShapeDtypeStruct((blocks, 128, 128)...  1 us

profile of v5, /device:TPU:1, one launch (start us, length us, event | category | flops | bytes accessed | tf_op | source)
XLA Modules:
  0.0 25.3 jit_solution(1914842242980467257)
XLA Ops:
  0.0 24.3 %shard_map.73.held = f32[13,128,128]{2,1,0:T(8,128)S(1)} custom-call(f32[2,2,128,128]{3,2,1,0:T(8,128)} %inv_h.1, f32[2,2,128]{2,1,0:T(2,128)} %vd_h.1, f32[2,2,128]{2,1,0:T(2,128)} %vc_h.1, f32[2,2,128]{2,1,0:T(2,128)} %fe_h.1, f32[2,2,128]{2,1,0:T(2,128)} %fn_h.1, s32[2,2]{1,0:T(2,128)} %land_h.1, s32[2,2]{1,0:T(2,128)} %agg_h.1), custom_call_target="tpu_custom_call" | custom-call | tf_op jit(solution)/shard_map/pallas_call | solution.py:581
  24.3 1.0 %shard_map.74 = f32[13,128,128]{2,1,0:T(8,128)} custom-call(f32[13,128,128]{2,1,0:T(8,128)S(1)} %shard_map.73.held), custom_call_target="tpu_custom_call" | custom-call | tf_op jit(solution)/shard_map/pallas_call | solution.py:601

commit v6 on v5

--- a/solution.py
+++ b/solution.py
@@ -100,7 +100,7 @@
     inv_h, vd_h, vc_h, fe_h, fn_h, land_h, agg_h,
     out,
     X, XC, PK, PC, SM, LA, PT, CF,
-    local_sem, send_sem, recv_sem,
+    local_sem, send_sem, recv_sem, ready,
 ):
     me_lon = lax.axis_index("lon")
     me_lat = lax.axis_index("lat")
@@ -179,6 +179,17 @@
                 XC[corner_blocks.index(block)] = jnp.zeros((128, 128), jnp.float32)
         pl.when(jnp.logical_not(exists(block)))(clear)
 
+    lat_near = jnp.where(inside[1], 1, 0) + jnp.where(inside[-1], 1, 0)
+    lat_second = jnp.where(inside[2], 1, 0) + jnp.where(inside[-2], 1, 0)
+    from_west = jnp.where(late, 0, 1 + lat_near) + jnp.where(phase > 1, 1, 0)
+    awaited_inner = lat_near + lat_second + from_west
+    awaited_rim = jnp.where(even, lat_near, 0) + jnp.where(inside[-2], 1, 0)
+    pl.semaphore_wait(barrier, 2 + lat_near + jnp.where(rim, awaited_rim, awaited_inner))
+
+    @pl.when(rim)
+    def _():
+        pl.semaphore_signal(ready, inc=1, device_id=target(east), device_id_type=MESH)
+
     for copy in small_copies:
         copy.wait()
     live = (LA[1] >= 0).astype(jnp.float32)
@@ -208,13 +219,6 @@
         for p in (0, 1):
             for r in (0, 1):
                 PK[0, pl.ds(first + 2 * p + r, 1), :] = mine(field, p, r)
-
-    lat_near = jnp.where(inside[1], 1, 0) + jnp.where(inside[-1], 1, 0)
-    lat_second = jnp.where(inside[2], 1, 0) + jnp.where(inside[-2], 1, 0)
-    from_west = jnp.where(late, 0, 1 + lat_near) + jnp.where(phase > 1, 1, 0)
-    awaited_inner = lat_near + lat_second + from_west
-    awaited_rim = jnp.where(even, lat_near, 0) + jnp.where(inside[-2], 1, 0)
-    pl.semaphore_wait(barrier, 2 + lat_near + jnp.where(rim, awaited_rim, awaited_inner))
 
     sends = []
 
@@ -527,11 +531,14 @@
         if block[0] > 0:
             corner(block)
 
+    @pl.when(late)
+    def _():
+        pl.semaphore_wait(ready, 1)
+
+    send_blocks(west, near_cells, late)
     for block in west_side + [(-2, 0)]:
         wait_packet(block, inner)
         send_packet(block, phase <= 1 if block == (-2, 0) else late)
-        if block == west:
-            send_blocks(west, near_cells, late)
     for cell in all_cells:
         if cell[0] <= 0:
             make_coefs(cell)
@@ -595,6 +602,7 @@
             pltpu.SemaphoreType.DMA((7,)),
             pltpu.SemaphoreType.DMA((messages,)),
             pltpu.SemaphoreType.DMA((messages,)),
+            pltpu.SemaphoreType.REGULAR,
         ],
         compiler_params=pltpu.CompilerParams(collective_id=0, has_side_effects=True),
     )(inverse, vert_diag, vert_coup, face_east, face_north, land_mask, aggregate)

time: 25.4 us -> 25.6 us (level)
  no operation moved by 1% of the time
where the time goes in v6:
time: 25.6 us; the launch traced here: 25.3 us
  Pallas kernels  25.3 us (99%)
    pallas_call x1, Pallas kernels, local(): pl.pallas_call(kernel, out_shape=pltpu.VMEM((blocks, 128, 128), jnp.float...  24.3 us
    pallas_call x1, Pallas kernels, local(): pl.pallas_call(publish, out_shape=jax.ShapeDtypeStruct((blocks, 128, 128)...  1 us

profile of v6, /device:TPU:1, one launch (start us, length us, event | category | flops | bytes accessed | tf_op | source)
XLA Modules:
  0.0 25.3 jit_solution(10387093903538473445)
XLA Ops:
  0.0 24.3 %shard_map.73.held = f32[13,128,128]{2,1,0:T(8,128)S(1)} custom-call(f32[2,2,128,128]{3,2,1,0:T(8,128)} %inv_h.1, f32[2,2,128]{2,1,0:T(2,128)} %vd_h.1, f32[2,2,128]{2,1,0:T(2,128)} %vc_h.1, f32[2,2,128]{2,1,0:T(2,128)} %fe_h.1, f32[2,2,128]{2,1,0:T(2,128)} %fn_h.1, s32[2,2]{1,0:T(2,128)} %land_h.1, s32[2,2]{1,0:T(2,128)} %agg_h.1), custom_call_target="tpu_custom_call" | custom-call | tf_op jit(solution)/shard_map/pallas_call | solution.py:588
  24.3 1.0 %shard_map.74 = f32[13,128,128]{2,1,0:T(8,128)} custom-call(f32[13,128,128]{2,1,0:T(8,128)S(1)} %shard_map.73.held), custom_call_target="tpu_custom_call" | custom-call | tf_op jit(solution)/shard_map/pallas_call | solution.py:609
